TPU v7x, 256 devices: a whole 4x4x8 slice. The times are simulated.
256 devices in a mesh: dp: 16 (over z_lo, y), mp: 16 (over x, z_hi, core).
Axes of the slice: x: 4, y: 4, z: 8 (z_hi: 2, z_lo: 4; z = z_hi * 4 + z_lo), core: 2. Of those that a mesh axis runs over, the one named last changes fastest.
Arguments:
- image_tokens: bfloat16 [16, 192, 3072], P('dp'), may hold values from -6 to 6
- text_tokens: bfloat16 [16, 64, 3072], P('dp'), may hold values from -6 to 6
- null_prompt: bfloat16 [64, 3072], replicated, may hold values from -6 to 6
- drop_flags: int32 [16], P('dp'), may hold values 0 or 1
- time_index: int32 [16], P('dp'), may hold values from 0 to 31
- modulation: float32 [32, 3, 3072], replicated, may hold values from -3 to 3
- w_up: bfloat16 [3072, 12288], P('dp', 'mp'), may hold values from -0.109375 to 0.109375
- w_down: bfloat16 [12288, 3072], P('mp', 'dp'), may hold values from -0.0546875 to 0.0546875
- d_output: bfloat16 [16, 256, 3072], P('dp'), may hold values from -6 to 6
Outputs:
- block_out: bfloat16 [16, 256, 3072], P('dp')
- d_tokens: bfloat16 [16, 256, 3072], P('dp')
- grad_up: float32 [3072, 12288], P('dp', 'mp')
- grad_down: float32 [12288, 3072], P('mp', 'dp')
- grad_null: float32 [64, 3072], replicated
All inputs are finite; a program needn't handle non-finite values. No bound on the sum of `drop_flags` on one device may be relied on, other than what follows from the above.
Results may differ from a plain program's by a relative error of at most 0.017.
Values may be sent and summed in bfloat16 or wider, within the bound.
No kernel may reach another device: no remote copies, remote signals or barrier semaphores. Data moves between devices by JAX's collectives and lax.ppermute only.
A program may use at most 128 MiB of HBM per device.

v0:
```python
import jax
import jax.numpy as jnp
from jax import lax
from jax.sharding import Mesh
from jax.sharding import PartitionSpec as P

MP = ("mp_0", "mp_1", "mp_2")


EPS = 1e-06


def rows_first(arrays, axis, dims):
    turned = [jnp.moveaxis(a, dim, 0) for a, dim in zip(arrays, dims)]
    both = jnp.concatenate([t.reshape(len(t), -1) for t in turned], axis=1)
    out, at, finished = (lax.all_gather(both, axis, axis=0, tiled=True), 0, [])
    for t, dim in zip(turned, dims):
        slab = out[:, at : at + t[0].size].reshape(-1, *t.shape[1:])
        finished.append(jnp.moveaxis(slab, 0, dim))
        at += t[0].size
    return tuple(finished)


def in_blocks(shard, dim, peers):
    before, after = (shard.shape[:dim], shard.shape[dim + 1 :])
    return jnp.moveaxis(shard.reshape(*before, peers, -1, *after), dim, 0)


def summed_on_arrival(shard, axis, dim):
    peers = lax.axis_size(axis)
    pieces = lax.all_to_all(in_blocks(shard, dim, peers), axis, 0, 0, tiled=True)
    return jnp.sum(pieces.astype(jnp.float32), axis=0)


def sum_in_two_steps(shard, axes, dim):
    far, near = axes
    own = summed_on_arrival(in_blocks(shard, dim, lax.axis_size(far)), near, dim + 1)
    return jnp.sum(
        lax.all_to_all(own.astype(jnp.bfloat16), far, 0, 0, tiled=True).astype(jnp.float32), axis=0
    )


def filled_up(lines, peers):
    spare = -len(lines) % peers
    return jnp.pad(lines, [(0, spare)] + [(0, 0)] * (lines.ndim - 1))


def sent_to_all(shard, axis):
    copies = jnp.broadcast_to(shard, (lax.axis_size(axis), *shard.shape))
    return lax.all_to_all(copies, axis, split_axis=0, concat_axis=0, tiled=True)


def in_order(pieces, dim):
    lengths = list(pieces.shape[1:])
    lengths[dim] *= pieces.shape[0]
    return jnp.moveaxis(pieces, 0, dim).reshape(lengths)


def gathered_by_axis(shard, axes, dim):
    far, near = axes
    leading = sent_to_all(shard, far)
    pieces = jnp.swapaxes(sent_to_all(leading, near), 0, 1)
    return in_order(pieces.reshape(-1, *shard.shape), dim)


def total_of(shard, axes):
    lines = shard.reshape(-1, shard.shape[-1])
    own = sum_in_two_steps(
        filled_up(lines, lax.axis_size(axes[0]) * lax.axis_size(axes[1])), axes, 0
    )
    whole = gathered_by_axis(own.astype(jnp.bfloat16), axes, 0)
    return whole[: len(lines)].reshape(shard.shape).astype(jnp.float32)


def collect(shard, axis, dim):
    pieces = sent_to_all(shard, axis)
    return in_order(pieces, dim)


def nested_sum(shard, axes):
    lines = shard.reshape(-1, shard.shape[-1])
    padded = filled_up(lines, lax.axis_size(axes))
    whole = collect(summed_on_arrival(padded, axes, 0).astype(jnp.bfloat16), axes, 0)
    return lax.slice_in_dim(whole, 0, len(lines)).reshape(shard.shape).astype(jnp.float32)


def gelu_tanh(values):
    return jax.nn.gelu(values, approximate=True)


def contract_rows(left, right):
    return lax.dot_general(
        left, right, (((0,), (0,)), ((), ())), preferred_element_type=jnp.float32
    )


def contract_cols(left, right):
    return lax.dot_general(
        left, right, (((1,), (1,)), ((), ())), preferred_element_type=jnp.float32
    )


def shards(
    image_tokens,
    text_tokens,
    null_prompt,
    drop_flags,
    time_index,
    modulation,
    w_up,
    w_down,
    d_output,
):
    dropped = drop_flags == 1
    text_in = jnp.where(dropped[:, None, None], null_prompt[None], text_tokens)
    joined = jnp.concatenate([text_in, image_tokens], axis=1)
    levels = jnp.arange(modulation.shape[0], dtype=jnp.int32)
    indicator_matrix = (time_index[:, None] == levels[None, :]).astype(jnp.float32)
    modulation_vectors = jnp.einsum(
        "yi,imr->ymr", indicator_matrix, modulation, precision=lax.Precision.HIGHEST
    )
    shift_modulation = modulation_vectors[:, 0][:, None]
    scale_mod = modulation_vectors[:, 1][:, None]
    gate_mod = modulation_vectors[:, 2][:, None]
    batch, length, width = joined.shape
    joined32 = joined.astype(jnp.float32)
    centred = joined32 - jnp.mean(joined32, axis=-1, keepdims=True)
    inv_std = lax.rsqrt(jnp.mean(centred * centred, axis=-1, keepdims=True) + EPS)
    normed = centred * inv_std
    mod_in = (normed * (1.0 + scale_mod) + shift_modulation).astype(jnp.bfloat16)
    flat_in = mod_in.reshape(batch * length, width)
    full_up, full_down = rows_first((w_up, w_down), "dp", (0, 1))
    preactivation_rows = jnp.dot(flat_in, full_up, preferred_element_type=jnp.float32)
    hidden = gelu_tanh(preactivation_rows).astype(jnp.bfloat16)
    partial_value = jnp.dot(hidden, full_down, preferred_element_type=jnp.float32)
    branch = total_of(partial_value.astype(jnp.bfloat16), (("mp_0", "mp_1"), "mp_2")).reshape(
        batch, length, width
    )
    block_out = (joined32 + gate_mod * branch).astype(jnp.bfloat16)
    d_out32 = d_output.astype(jnp.float32)
    d_branch = (d_out32 * gate_mod).astype(jnp.bfloat16).reshape(batch * length, width)
    hidden_gradient = contract_cols(d_branch, full_down)
    _, gelu_back = jax.vjp(gelu_tanh, preactivation_rows)
    d_pre = gelu_back(hidden_gradient)[0].astype(jnp.bfloat16)
    d_part = contract_cols(d_pre, full_up)
    d_mod = total_of(d_part.astype(jnp.bfloat16), (("mp_0", "mp_1"), "mp_2"))
    hid_local = w_up.shape[1]
    both = lax.psum_scatter(
        jnp.concatenate(
            [contract_rows(flat_in, d_pre), contract_rows(d_branch, hidden)], axis=1
        ).astype(jnp.bfloat16),
        "dp",
        scatter_dimension=0,
        tiled=True,
    ).astype(jnp.float32)
    grad_up = both[:, :hid_local]
    grad_down = both[:, hid_local:].T
    d_normed = d_mod.reshape(batch, length, width) * (1.0 + scale_mod)
    d_full = d_out32 + inv_std * (
        d_normed
        - jnp.mean(d_normed, axis=-1, keepdims=True)
        - normed * jnp.mean(d_normed * normed, axis=-1, keepdims=True)
    )
    text_len = null_prompt.shape[0]
    null_part = jnp.sum(
        jnp.where(dropped[:, None, None], d_full[:, :text_len], jnp.float32(0.0)), axis=0
    )
    grad_null = nested_sum(null_part.astype(jnp.bfloat16), "dp")
    return (block_out, d_full.astype(jnp.bfloat16), grad_up, grad_down, grad_null)


def solution(mesh):
    torus = Mesh(mesh.devices.reshape(mesh.shape["dp"], 4, 2, 2), ("dp", "mp_0", "mp_1", "mp_2"))
    in_specs = (
        P("dp", None, None),
        P("dp", None, None),
        P(),
        P("dp"),
        P("dp"),
        P(),
        P("dp", MP),
        P(MP, "dp"),
        P("dp", None, None),
    )
    out_specs = (P("dp", None, None), P("dp", None, None), P("dp", MP), P(MP, "dp"), P())
    return jax.shard_map(
        shards, mesh=torus, in_specs=in_specs, out_specs=out_specs, check_vma=False
    )
```

profile of v0, /device:TPU:32, one launch (start us, length us, event | category | flops | bytes accessed | tf_op | source)
XLA Modules:
  0.0 438.3 jit_solution(4670006479113988557)
XLA Ops:
  7.2 2.1 pad_maximum_fusion.2
  10.7 1.0 bitcast_select_fusion
  13.1 109.8 %all-gather.2.cloned.1.call-done = bf16[3072,1536]{1,0:T(8,128)(2,1)} async-done(((bf16[192,1536]{1,0:T(8,128)(2,1)}), bf16[3072,1536]{1,0:T(8,128)(2,1)}) %all-gather.2.cloned.1.call-update) | async-done | bytes 9437200 | tf_op jit(solution)/shard_map/all_gather | solution.py:16
  122.9 4.1 fusion.6
  127.0 1.6 convolution_convert_fusion
  128.7 1.7 fusion.25
  130.4 1.6 convolution_convert_fusion.1
  132.0 4.7 %pad_maximum_fusion = bf16[3072,1536]{0,1:T(8,128)(2,1)} fusion(bf16[3072,768]{0,1:T(8,128)(2,1)S(1)} %convolution_convert_fusion, bf16[3072,768]{0,1:T(8,128)(2,1)S(1)} %convolution_convert_fusion.1), kind=kLoop, calls=%fused_computation | loop fusion | flops 18874368 | bytes 18874368 | tf_op jit(solution)/shard_map/concatenate | solution.py:149
  136.7 12.7 %copy.33 = bf16[3072,1536]{1,0:T(8,128)(2,1)} copy(bf16[3072,1536]{0,1:T(8,128)(2,1)} %pad_maximum_fusion) | data formatting | bytes 18874368
  149.4 3.8 fusion.11
  153.3 1.3 copy.47
  154.6 4.6 %all-to-all-start = ((bf16[2,8,16,3072]{3,2,1,0:T(8,128)(2,1)}), bf16[2,8,16,3072]{3,2,1,0:T(8,128)(2,1)}, u32[]{:S(2)}, u32[]{:S(2)}) async-start(bf16[2,8,16,3072]{3,2,1,0:T(8,128)(2,1)} %bitcast.63), calls=%async_computation | async-start | bytes 3145728 | tf_op jit(solution)/shard_map/all_to_all | solution.py:31
  159.2 4.2 fusion.8
  163.3 1.3 copy.46
  164.6 4.6 %all-to-all-start.4 = ((bf16[2,8,16,3072]{3,2,1,0:T(8,128)(2,1)}), bf16[2,8,16,3072]{3,2,1,0:T(8,128)(2,1)}, u32[]{:S(2)}, u32[]{:S(2)}) async-start(bf16[2,8,16,3072]{3,2,1,0:T(8,128)(2,1)} %bitcast.62), calls=%async_computation.4 | async-start | bytes 3145728 | tf_op jit(solution)/shard_map/all_to_all | solution.py:31
  169.2 2.8 reduce_sum.102
  172.1 9.4 %all-to-all-start.1 = ((bf16[8,16,3072]{2,1,0:T(8,128)(2,1)}), bf16[8,16,3072]{2,1,0:T(8,128)(2,1)S(1)}, u32[]{:S(2)}, u32[]{:S(2)}) async-start(bf16[8,16,3072]{2,1,0:T(8,128)(2,1)} %reduce_sum.102), calls=%async_computation.1 | async-start | bytes 1572864 | tf_op jit(solution)/shard_map/all_to_all | solution.py:39
  181.4 2.8 reduce_sum.104
  184.3 31.8 %all-to-all-done.1 = bf16[8,16,3072]{2,1,0:T(8,128)(2,1)S(1)} async-done(((bf16[8,16,3072]{2,1,0:T(8,128)(2,1)}), bf16[8,16,3072]{2,1,0:T(8,128)(2,1)S(1)}, u32[]{:S(2)}, u32[]{:S(2)}) %all-to-all-start.1) | async-done | bytes 786464 | tf_op jit(solution)/shard_map/all_to_all | solution.py:39
  216.1 3.6 all-to-all-start.5
  219.7 33.8 %all-to-all-done.5 = bf16[8,16,3072]{2,1,0:T(8,128)(2,1)S(1)} async-done(((bf16[8,16,3072]{2,1,0:T(8,128)(2,1)}), bf16[8,16,3072]{2,1,0:T(8,128)(2,1)S(1)}, u32[]{:S(2)}, u32[]{:S(2)}) %all-to-all-start.5) | async-done | bytes 786464 | tf_op jit(solution)/shard_map/all_to_all | solution.py:39
  253.6 1.0 broadcast_in_dim.49
  254.5 3.5 all-to-all-start.2
  258.2 33.1 %all-to-all-done.2 = bf16[8,16,3072]{2,1,0:T(8,128)(2,1)S(1)} async-done(((bf16[8,16,3072]{2,1,0:T(8,128)(2,1)}), bf16[8,16,3072]{2,1,0:T(8,128)(2,1)S(1)}, u32[]{:S(2)}, u32[]{:S(2)}) %all-to-all-start.2) | async-done | bytes 786464 | tf_op jit(solution)/shard_map/all_to_all | solution.py:50
  291.3 1.0 broadcast_in_dim.51
  292.2 3.5 all-to-all-start.6
  296.0 2.0 fusion.37
  298.0 30.2 %all-to-all-done.6 = bf16[8,16,3072]{2,1,0:T(8,128)(2,1)S(1)} async-done(((bf16[8,16,3072]{2,1,0:T(8,128)(2,1)}), bf16[8,16,3072]{2,1,0:T(8,128)(2,1)S(1)}, u32[]{:S(2)}, u32[]{:S(2)}) %all-to-all-start.6) | async-done | bytes 786464 | tf_op jit(solution)/shard_map/all_to_all | solution.py:50
  328.4 5.9 %all_to_all.50 = bf16[2,8,16,3072]{3,2,1,0:T(8,128)(2,1)} all-to-all(bf16[2,8,16,3072]{3,2,1,0:T(8,128)(2,1)S(1)} %broadcast_in_dim.52), channel_id=1, replica_groups=mesh['dp'=16,'mp_0'=4,'mp_1'=2,'mp_2'=2] {'mp_2'}, dimensions={0} | all-to-all | bytes 3145728 | tf_op jit(solution)/shard_map/all_to_all | solution.py:50
  334.2 1.3 broadcast_in_dim.50
  335.6 4.7 %all-to-all-start.3 = ((bf16[2,8,16,3072]{3,2,1,0:T(8,128)(2,1)}), bf16[2,8,16,3072]{3,2,1,0:T(8,128)(2,1)}, u32[]{:S(2)}, u32[]{:S(2)}) async-start(bf16[2,8,16,3072]{3,2,1,0:T(8,128)(2,1)} %broadcast_in_dim.50), calls=%async_computation.3 | async-start | bytes 3145728 | tf_op jit(solution)/shard_map/all_to_all | solution.py:50
  340.2 3.5 bitcast_reduce_fusion
  343.9 1.8 copy_convert_fusion
  345.7 3.0 convert_add_fusion
  348.8 1.1 copy-done.4
  350.0 0.9 convert_element_type.161
  350.9 43.4 %all-to-all-start.8 = ((bf16[16,4,3072]{2,1,0:T(4,128)(2,1)}), bf16[16,4,3072]{2,1,0:T(4,128)(2,1)S(1)}, u32[]{:S(2)}, u32[]{:S(2)}) async-start(bf16[16,4,3072]{2,1,0:T(4,128)(2,1)} %convert_element_type.161), calls=%async_computation.8 | async-start | bytes 786432 | tf_op jit(solution)/shard_map/all_to_all | solution.py:31
  394.2 3.4 copy_convert_fusion.1
  397.6 9.3 %all-to-all-done.8 = bf16[16,4,3072]{2,1,0:T(4,128)(2,1)S(1)} async-done(((bf16[16,4,3072]{2,1,0:T(4,128)(2,1)}), bf16[16,4,3072]{2,1,0:T(4,128)(2,1)S(1)}, u32[]{:S(2)}, u32[]{:S(2)}) %all-to-all-start.8) | async-done | bytes 393248 | tf_op jit(solution)/shard_map/all_to_all | solution.py:31
  408.0 5.1 %all-to-all-start.9 = ((bf16[16,4,3072]{2,1,0:T(4,128)(2,1)}), bf16[16,4,3072]{2,1,0:T(4,128)(2,1)S(1)}, u32[]{:S(2)}, u32[]{:S(2)}) async-start(bf16[16,4,3072]{2,1,0:T(4,128)(2,1)} %broadcast_in_dim.54), calls=%async_computation.9 | async-start | bytes 786432 | tf_op jit(solution)/shard_map/all_to_all | solution.py:50
  413.1 3.5 add_convert_fusion
  416.6 7.9 %all-to-all-done.9 = bf16[16,4,3072]{2,1,0:T(4,128)(2,1)S(1)} async-done(((bf16[16,4,3072]{2,1,0:T(4,128)(2,1)}), bf16[16,4,3072]{2,1,0:T(4,128)(2,1)S(1)}, u32[]{:S(2)}, u32[]{:S(2)}) %all-to-all-start.9) | async-done | bytes 393248 | tf_op jit(solution)/shard_map/all_to_all | solution.py:50
  424.5 0.9 reshape.496
  425.4 1.3 copy.34
  426.8 1.3 convert_element_type.159
  428.1 1.1 copy.30
  429.2 1.2 slice_bitcast_fusion
  430.4 1.1 copy.31
  (43 shorter events, 3.5 us)
Async XLA Ops:
  7.2 5.4 %copy-start = (f32[32,3,3072]{2,0,1:T(8,128)S(1)}, f32[32,3,3072]{2,0,1:T(8,128)}, u32[]{:S(2)}) copy-start(f32[32,3,3072]{2,0,1:T(8,128)} %param.14) | copy-start | bytes 3538948
  7.2 4.5 %copy-start.2 = (bf16[1,192,3072]{2,1,0:T(8,128)(2,1)S(1)}, bf16[1,192,3072]{2,1,0:T(8,128)(2,1)}, u32[]{:S(2)}) copy-start(bf16[1,192,3072]{2,1,0:T(8,128)(2,1)} %param.9) | copy-start | bytes 3538948
  7.2 115.7 %all-gather.2.cloned.1.call-start = ((), (), s32[]{:S(2)}) async-start(), calls=%async_computation.11 | async-start | bytes 10027008 | tf_op jit(solution)/shard_map/all_gather | solution.py:16
  9.3 416.1 %reduce-scatter.4.cloned.1.call-start = ((), (), s32[]{:S(2)}) async-start(), calls=%async_computation.12 | async-start | bytes 10027008
  122.9 4.1 copy-start.3
  122.9 5.7 %slice-start = ((s8[9437184]{0:T(1024)(128)(4,1)}), s8[4194304]{0:T(1024)(128)(4,1)S(1)}, s32[]{:S(2)}) async-start(s8[9437184]{0:T(1024)(128)(4,1)} %bitcast.76), calls=%async_computation.13 | async-start | bytes 8388608
  122.9 5.7 %slice-start.1 = ((s8[9437184]{0:T(1024)(128)(4,1)}), s8[4194304]{0:T(1024)(128)(4,1)S(1)}, s32[]{:S(2)}) async-start(s8[9437184]{0:T(1024)(128)(4,1)} %bitcast.76), calls=%async_computation.14 | async-start | bytes 8388608
  127.0 1.7 slice-start.2
  154.6 10.1 %all-to-all-start = ((bf16[2,8,16,3072]{3,2,1,0:T(8,128)(2,1)}), bf16[2,8,16,3072]{3,2,1,0:T(8,128)(2,1)}, u32[]{:S(2)}, u32[]{:S(2)}) async-start(bf16[2,8,16,3072]{3,2,1,0:T(8,128)(2,1)} %bitcast.63), calls=%async_computation | async-start | bytes 3145728 | tf_op jit(solution)/shard_map/all_to_all | solution.py:31
  164.6 7.5 %all-to-all-start.4 = ((bf16[2,8,16,3072]{3,2,1,0:T(8,128)(2,1)}), bf16[2,8,16,3072]{3,2,1,0:T(8,128)(2,1)}, u32[]{:S(2)}, u32[]{:S(2)}) async-start(bf16[2,8,16,3072]{3,2,1,0:T(8,128)(2,1)} %bitcast.62), calls=%async_computation.4 | async-start | bytes 3145728 | tf_op jit(solution)/shard_map/all_to_all | solution.py:31
  172.1 44.0 %all-to-all-start.1 = ((bf16[8,16,3072]{2,1,0:T(8,128)(2,1)}), bf16[8,16,3072]{2,1,0:T(8,128)(2,1)S(1)}, u32[]{:S(2)}, u32[]{:S(2)}) async-start(bf16[8,16,3072]{2,1,0:T(8,128)(2,1)} %reduce_sum.102), calls=%async_computation.1 | async-start | bytes 1572864 | tf_op jit(solution)/shard_map/all_to_all | solution.py:39
  216.1 37.5 %all-to-all-start.5 = ((bf16[8,16,3072]{2,1,0:T(8,128)(2,1)}), bf16[8,16,3072]{2,1,0:T(8,128)(2,1)S(1)}, u32[]{:S(2)}, u32[]{:S(2)}) async-start(bf16[8,16,3072]{2,1,0:T(8,128)(2,1)} %reduce_sum.104), calls=%async_computation.5 | async-start | bytes 1572864 | tf_op jit(solution)/shard_map/all_to_all | solution.py:39
  254.5 36.8 %all-to-all-start.2 = ((bf16[8,16,3072]{2,1,0:T(8,128)(2,1)}), bf16[8,16,3072]{2,1,0:T(8,128)(2,1)S(1)}, u32[]{:S(2)}, u32[]{:S(2)}) async-start(bf16[8,16,3072]{2,1,0:T(8,128)(2,1)} %broadcast_in_dim.49), calls=%async_computation.2 | async-start | bytes 1572864 | tf_op jit(solution)/shard_map/all_to_all | solution.py:50
  292.2 35.9 %all-to-all-start.6 = ((bf16[8,16,3072]{2,1,0:T(8,128)(2,1)}), bf16[8,16,3072]{2,1,0:T(8,128)(2,1)S(1)}, u32[]{:S(2)}, u32[]{:S(2)}) async-start(bf16[8,16,3072]{2,1,0:T(8,128)(2,1)} %broadcast_in_dim.51), calls=%async_computation.6 | async-start | bytes 1572864 | tf_op jit(solution)/shard_map/all_to_all | solution.py:50
  335.6 15.3 %all-to-all-start.3 = ((bf16[2,8,16,3072]{3,2,1,0:T(8,128)(2,1)}), bf16[2,8,16,3072]{3,2,1,0:T(8,128)(2,1)}, u32[]{:S(2)}, u32[]{:S(2)}) async-start(bf16[2,8,16,3072]{3,2,1,0:T(8,128)(2,1)} %broadcast_in_dim.50), calls=%async_computation.3 | async-start | bytes 3145728 | tf_op jit(solution)/shard_map/all_to_all | solution.py:50
  348.7 1.1 copy-start.4
  350.9 56.1 %all-to-all-start.8 = ((bf16[16,4,3072]{2,1,0:T(4,128)(2,1)}), bf16[16,4,3072]{2,1,0:T(4,128)(2,1)S(1)}, u32[]{:S(2)}, u32[]{:S(2)}) async-start(bf16[16,4,3072]{2,1,0:T(4,128)(2,1)} %convert_element_type.161), calls=%async_computation.8 | async-start | bytes 786432 | tf_op jit(solution)/shard_map/all_to_all | solution.py:31
  408.0 16.5 %all-to-all-start.9 = ((bf16[16,4,3072]{2,1,0:T(4,128)(2,1)}), bf16[16,4,3072]{2,1,0:T(4,128)(2,1)S(1)}, u32[]{:S(2)}, u32[]{:S(2)}) async-start(bf16[16,4,3072]{2,1,0:T(4,128)(2,1)} %broadcast_in_dim.54), calls=%async_computation.9 | async-start | bytes 786432 | tf_op jit(solution)/shard_map/all_to_all | solution.py:50
  426.8 4.7 %copy-start.1 = (f32[32,3,3072]{2,0,1:T(8,128)S(1)}, f32[32,3,3072]{2,0,1:T(8,128)}, u32[]{:S(2)}) copy-start(f32[32,3,3072]{2,0,1:T(8,128)} %param.14) | copy-start | bytes 3538948
Sparse Core Ops, SparseCore 0:
  10.4 112.4 all-gather.1
  149.6 177.3 reduce-scatter.3
where the time goes:
time: 440 us; the launch traced here: 438 us
  waiting for transfers between devices  256 us (58%)
  starting transfers between devices  82.5 us (19%)
  other arithmetic  33.3 us (8%)
  local copies, waits for them, and re-layouts  27.6 us (6%)
  matrix products  17.5 us (4%)
  between operations  15.6 us (4%)
  blocking collectives  5.86 us (1%)
    all_gather x1, waiting for transfers between devices, rows_first(): out, at, finished = (lax.all_gather(both, axis, axis=0, tiled=True), 0, [])  110 us
    all_to_all x4, waiting for transfers between devices, sent_to_all(): return lax.all_to_all(copies, axis, split_axis=0, concat_axis=0, tiled=True)  71.2 us
    all_to_all x2, waiting for transfers between devices, sum_in_two_steps(): lax.all_to_all(own.astype(jnp.bfloat16), far, 0, 0, tiled=True)  65.6 us
    all_to_all x3, starting transfers between devices, summed_on_arrival(): lax.all_to_all(in_blocks(shard, dim, peers), axis, 0, 0, tiled=True)  52.6 us
    unnamed x20, local copies, waits for them, and re-layouts  17.4 us
    all_to_all x4, starting transfers between devices, sent_to_all(): return lax.all_to_all(copies, axis, split_axis=0, concat_axis=0, tiled=True)  16.9 us
    all_to_all x2, starting transfers between devices, sum_in_two_steps(): lax.all_to_all(own.astype(jnp.bfloat16), far, 0, 0, tiled=True)  12.9 us
    all_to_all x3, waiting for transfers between devices, summed_on_arrival(): lax.all_to_all(in_blocks(shard, dim, peers), axis, 0, 0, tiled=True)  9.3 us
  transfers between devices with their start and end apart: 11, of which 7 were waited for; matrix products, arithmetic and copies ran while one was open for 10% of the time, Pallas kernels for 0%

commit v1 on v0

v1 whole, which is shorter than its diff:
```python
import jax
import jax.numpy as jnp
from jax import lax
from jax.sharding import Mesh
from jax.sharding import PartitionSpec as P

EPS = 1e-06

G = 2

Z = ("zq", "zp")
DP = ("zq", "zp", "y")
MP = ("x", "zh", "c")
SLOT = ("c", "x")
NZ = 4
NY = 4


def exchange(pieces, axes):
    return lax.all_to_all(pieces, axes, 0, 0, tiled=True)


def spread(piece, axes, count):
    if count == 1:
        return piece[None]
    return exchange(jnp.broadcast_to(piece[None], (count, *piece.shape)), axes)


def summed(pieces):
    return jnp.sum(pieces.astype(jnp.float32), axis=0)


def gelu_tanh(values):
    return jax.nn.gelu(values, approximate=True)


def contract_rows(left, right):
    return lax.dot_general(
        left, right, (((0,), (0,)), ((), ())), preferred_element_type=jnp.float32
    )


def contract_cols(left, right):
    return lax.dot_general(
        left, right, (((1,), (1,)), ((), ())), preferred_element_type=jnp.float32
    )


def y_first(rows):
    n, d = rows.shape
    return rows.reshape(n, NZ, NY, -1).swapaxes(1, 2).reshape(n, d)


def z_first(rows):
    n, d = rows.shape
    return rows.reshape(n, NY, NZ, -1).swapaxes(1, 2).reshape(n, d)


def part_weights(weight):
    rows, hid = weight.shape
    cut = [weight[:, at : at + hid // G] for at in range(0, hid, hid // G)]
    sent = jnp.stack(cut * (NZ // G))
    got = exchange(sent, Z).reshape(NZ * rows, hid // G)
    return lax.all_gather(got, "y", axis=0, tiled=True)


def own_grads(grad):
    hid = grad.shape[1]
    mine = lax.psum_scatter(grad.astype(jnp.bfloat16), "y", scatter_dimension=0, tiled=True)
    rows = mine.shape[0] // NZ
    got = exchange(mine.reshape(NZ, rows, hid), Z).reshape(NZ // G, G, rows, hid)
    return jnp.concatenate([summed(got[:, part]) for part in range(G)], axis=1)


def own_slot(part):
    width = part.shape[1]
    half = summed(exchange(part.reshape(2, -1, width), "c")).astype(jnp.bfloat16)
    slot = summed(exchange(half.reshape(4, -1, width), "x")).astype(jnp.bfloat16)
    both = slot.reshape(G, 1, -1, width)
    both = jnp.broadcast_to(both, (G, 2, *both.shape[2:])).reshape(2 * G, -1, width)
    return z_first(summed(exchange(both, ("zp", "zh"))))


def whole_sample(slot, text):
    every = spread(slot, SLOT, 8)
    width = slot.shape[1]
    return jnp.concatenate(
        [every[:, :text].reshape(-1, width), every[:, text:].reshape(-1, width)], axis=0
    )[None]


def shards(
    image_tokens,
    text_tokens,
    null_prompt,
    drop_flags,
    time_index,
    modulation,
    w_up,
    w_down,
    d_output,
):
    width = null_prompt.shape[1]
    text_len = null_prompt.shape[0]
    text = text_len // 8
    image = image_tokens.shape[1] // 8
    place = lax.axis_index(SLOT)
    dropped = drop_flags[0] == 1

    full_up = part_weights(w_up)
    full_down = part_weights(w_down.T)

    def rows_of(array, start, count):
        return lax.dynamic_slice_in_dim(array, start, count, 0)

    joined32 = jnp.concatenate(
        [
            jnp.where(
                dropped,
                rows_of(null_prompt, place * text, text),
                rows_of(text_tokens[0], place * text, text),
            ),
            rows_of(image_tokens[0], place * image, image),
        ],
        axis=0,
    ).astype(jnp.float32)
    d_out32 = jnp.concatenate(
        [
            rows_of(d_output[0], place * text, text),
            rows_of(d_output[0], text_len + place * image, image),
        ],
        axis=0,
    ).astype(jnp.float32)
    vectors = lax.dynamic_index_in_dim(modulation, time_index[0], 0, keepdims=False)
    shift, scale, gate = vectors[0][None], vectors[1][None], vectors[2][None]
    centred = joined32 - jnp.mean(joined32, axis=-1, keepdims=True)
    inv_std = lax.rsqrt(jnp.mean(centred * centred, axis=-1, keepdims=True) + EPS)
    normed = centred * inv_std
    mod_slot = y_first((normed * (1.0 + scale) + shift).astype(jnp.bfloat16))
    back_slot = y_first((d_out32 * gate).astype(jnp.bfloat16))

    pair = spread(jnp.stack([mod_slot, back_slot]), "zp", G)
    mod_in = spread(pair[:, 0], SLOT, 8).reshape(-1, width)
    d_branch = spread(pair[:, 1], SLOT, 8).reshape(-1, width)

    pre = jnp.dot(mod_in, full_up, preferred_element_type=jnp.float32)
    hidden = gelu_tanh(pre).astype(jnp.bfloat16)
    grad_down = own_grads(contract_rows(d_branch, hidden)).T
    hidden_gradient = jnp.dot(d_branch, full_down, preferred_element_type=jnp.float32)
    _, gelu_back = jax.vjp(gelu_tanh, pre)
    d_pre = gelu_back(hidden_gradient)[0].astype(jnp.bfloat16)
    grad_up = own_grads(contract_rows(mod_in, d_pre))

    branch = own_slot(contract_cols(hidden, full_down).astype(jnp.bfloat16))
    block_out = whole_sample((joined32 + gate * branch).astype(jnp.bfloat16), text)

    d_mod = own_slot(contract_cols(d_pre, full_up).astype(jnp.bfloat16))
    d_normed = d_mod * (1.0 + scale)
    d_full = d_out32 + inv_std * (
        d_normed
        - jnp.mean(d_normed, axis=-1, keepdims=True)
        - normed * jnp.mean(d_normed * normed, axis=-1, keepdims=True)
    )
    d_tokens = whole_sample(d_full.astype(jnp.bfloat16), text)

    null_part = jnp.where(dropped, d_full[:text], jnp.float32(0.0)).astype(jnp.bfloat16)
    null_part = null_part.reshape(text, 16, -1).swapaxes(0, 1)
    null_own = summed(exchange(null_part, DP)).astype(jnp.bfloat16)
    null_rows = spread(null_own, DP, 16).swapaxes(0, 1).reshape(text, width)
    grad_null = spread(null_rows, SLOT, 8).reshape(text_len, width).astype(jnp.float32)
    return (block_out, d_tokens, grad_up, grad_down, grad_null)


def solution(mesh):
    torus = Mesh(
        mesh.devices.reshape(NZ // G, G, NY, 4, 2, 2), ("zq", "zp", "y", "x", "zh", "c")
    )
    in_specs = (
        P(DP, None, None),
        P(DP, None, None),
        P(),
        P(DP),
        P(DP),
        P(),
        P(DP, MP),
        P(MP, DP),
        P(DP, None, None),
    )
    out_specs = (P(DP, None, None), P(DP, None, None), P(DP, MP), P(MP, DP), P())
    return jax.shard_map(
        shards, mesh=torus, in_specs=in_specs, out_specs=out_specs, check_vma=False
    )
```

time: 440 us -> 433 us (0.984)
  waiting for transfers between devices: 256 us -> 204 us
  blocking collectives: 5.86 us -> 43.2 us
  matrix products: 17.5 us -> 27.6 us
  other arithmetic: 33.3 us -> 25.5 us
  local copies, waits for them, and re-layouts: 27.6 us -> 32.8 us
    all_gather x1 -> x2, waiting for transfers between devices: 110 us -> 0.02 us  [part_weights(): return lax.all_gather(got, 'y', axis=0, tiled=True)]
    all_to_all x9 -> x15, waiting for transfers between devices: 146 us -> 203 us  [exchange(): return lax.all_to_all(pieces, axes, 0, 0, tiled=True)]
    all_to_all x1 -> x3, blocking collectives: 5.86 us -> 43.2 us  [exchange(): return lax.all_to_all(pieces, axes, 0, 0, tiled=True)]
    unnamed x20 -> x36, local copies, waits for them, and re-layouts: 17.4 us -> 0.95 us
    reshape x0 -> x9, local copies, waits for them, and re-layouts: none -> 11.3 us  [the longest x5 7.4 us: z_first(): return rows.reshape(n, NY, NZ, -1).swapaxes(1, 2).reshape(n, d)]
    convert_element_type x6 -> x3, other arithmetic: 12 us -> 1.62 us  [the longest x1 0.93 us: shards(): spread(null_rows, SLOT, 8).reshape(text_len, width).astype(jnp.float32)]
    broadcast_in_dim x5 -> x11, local copies, waits for them, and re-layouts: 4.27 us -> 12.8 us  [the longest x9 10.9 us: spread(): return exchange(jnp.broadcast_to(piece[None], (count, *piece.shape)), axes)]
    dot_general x2, matrix products: 3.22 us -> 10.5 us  [contract_rows(): lax.dot_general(left, right, (((0,), (0,)), ((), ())), preferred_element_...]
  transfers between devices with their start and end apart: 11 -> 19, of which waited for: 7 -> 14; matrix products, arithmetic and copies ran while one was open for 10% -> 16% of each run, Pallas kernels for 0% -> 0%
where the time goes in v1:
time: 433 us; the launch traced here: 427 us
  waiting for transfers between devices  204 us (47%)
  starting transfers between devices  78.2 us (18%)
  blocking collectives  43.2 us (10%)
  local copies, waits for them, and re-layouts  32.8 us (8%)
  matrix products  27.6 us (6%)
  other arithmetic  25.5 us (6%)
  between operations  15.5 us (4%)
    all_to_all x15, waiting for transfers between devices, exchange(): return lax.all_to_all(pieces, axes, 0, 0, tiled=True)  203 us
    all_to_all x15, starting transfers between devices, exchange(): return lax.all_to_all(pieces, axes, 0, 0, tiled=True)  78.2 us
    all_to_all x3, blocking collectives, exchange(): return lax.all_to_all(pieces, axes, 0, 0, tiled=True)  43.2 us
    reduce_sum x9, other arithmetic, summed(): return jnp.sum(pieces.astype(jnp.float32), axis=0)  11.4 us
    broadcast_in_dim x9, local copies, waits for them, and re-layouts, spread(): return exchange(jnp.broadcast_to(piece[None], (count, *piece.shape)), axes)  10.9 us
    dot_general x2, matrix products, contract_rows(): lax.dot_general(left, right, (((0,), (0,)), ((), ())), preferred_element_...  10.5 us
  transfers between devices with their start and end apart: 19, of which 14 were waited for; matrix products, arithmetic and copies ran while one was open for 16% of the time, Pallas kernels for 0%

profile of v1, /device:TPU:32, one launch (start us, length us, event | category | flops | bytes accessed | tf_op | source)
XLA Modules:
  0.0 427.4 jit_solution(13845521238257846741)
XLA Ops:
  9.2 6.0 %all-to-all-start.3 = ((bf16[4,192,384]{2,1,0:T(8,128)(2,1)}), bf16[4,192,384]{2,1,0:T(8,128)(2,1)S(1)}, u32[]{:S(2)}, u32[]{:S(2)}) async-start(bf16[4,192,384]{2,1,0:T(8,128)(2,1)} %pad_maximum_fusion.1), calls=%async_computation.3 | async-start | bytes 1179648 | tf_op jit(solution)/shard_map/all_to_all | solution.py:20
  20.6 2.3 fusion.18
  24.9 2.9 all-to-all-done.3
  28.9 6.8 %all-to-all-start = ((bf16[2,2,32,3072]{3,2,1,0:T(8,128)(2,1)}), bf16[2,2,32,3072]{3,2,1,0:T(8,128)(2,1)S(1)}, u32[]{:S(2)}, u32[]{:S(2)}) async-start(bf16[2,2,32,3072]{3,2,1,0:T(8,128)(2,1)} %broadcast_in_dim.36), calls=%async_computation | async-start | bytes 1572864 | tf_op jit(solution)/shard_map/all_to_all | solution.py:20
  38.3 6.0 %all-to-all-done = bf16[2,2,32,3072]{3,2,1,0:T(8,128)(2,1)S(1)} async-done(((bf16[2,2,32,3072]{3,2,1,0:T(8,128)(2,1)}), bf16[2,2,32,3072]{3,2,1,0:T(8,128)(2,1)S(1)}, u32[]{:S(2)}, u32[]{:S(2)}) %all-to-all-start) | async-done | bytes 786464 | tf_op jit(solution)/shard_map/all_to_all | solution.py:20
  44.3 5.2 %all-to-all-start.2 = ((bf16[4,192,384]{2,1,0:T(8,128)(2,1)}), bf16[4,192,384]{2,1,0:T(8,128)(2,1)S(1)}, u32[]{:S(2)}, u32[]{:S(2)}) async-start(bf16[4,192,384]{2,1,0:T(8,128)(2,1)} %pad_maximum_fusion), calls=%async_computation.2 | async-start | bytes 1179648 | tf_op jit(solution)/shard_map/all_to_all | solution.py:20
  50.4 10.4 %all-to-all-done.2 = bf16[4,192,384]{2,1,0:T(8,128)(2,1)S(1)} async-done(((bf16[4,192,384]{2,1,0:T(8,128)(2,1)}), bf16[4,192,384]{2,1,0:T(8,128)(2,1)S(1)}, u32[]{:S(2)}, u32[]{:S(2)}) %all-to-all-start.2) | async-done | bytes 589856 | tf_op jit(solution)/shard_map/all_to_all | solution.py:20
  60.8 3.2 broadcast_in_dim.81
  64.0 4.6 %all-to-all-start.8 = ((bf16[8,2,32,3072]{3,2,1,0:T(8,128)(2,1)}), bf16[8,2,32,3072]{3,2,1,0:T(8,128)(2,1)}, u32[]{:S(2)}, u32[]{:S(2)}) async-start(bf16[8,2,32,3072]{3,2,1,0:T(8,128)(2,1)} %broadcast_in_dim.81), calls=%async_computation.8 | async-start | bytes 6291456 | tf_op jit(solution)/shard_map/all_to_all | solution.py:20
  69.4 37.0 %all-to-all-done.8 = bf16[8,2,32,3072]{3,2,1,0:T(8,128)(2,1)} async-done(((bf16[8,2,32,3072]{3,2,1,0:T(8,128)(2,1)}), bf16[8,2,32,3072]{3,2,1,0:T(8,128)(2,1)}, u32[]{:S(2)}, u32[]{:S(2)}) %all-to-all-start.8) | async-done | bytes 3145760 | tf_op jit(solution)/shard_map/all_to_all | solution.py:20
  106.4 2.1 broadcast_in_dim.38
  108.5 4.4 %all-to-all-start.1 = ((bf16[8,2,32,3072]{3,2,1,0:T(8,128)(2,1)}), bf16[8,2,32,3072]{3,2,1,0:T(8,128)(2,1)}, u32[]{:S(2)}, u32[]{:S(2)}) async-start(bf16[8,2,32,3072]{3,2,1,0:T(8,128)(2,1)} %broadcast_in_dim.38), calls=%async_computation.1 | async-start | bytes 6291456 | tf_op jit(solution)/shard_map/all_to_all | solution.py:20
  113.0 4.4 %fusion.20 = f32[512,384]{1,0:T(8,128)S(1)} fusion(bf16[512,3072]{1,0:T(8,128)(2,1)} %bitcast.27, bf16[3072,384]{1,0:T(8,128)(2,1)} %all-gather.5.cloned.1.call-done), kind=kOutput, calls=%fused_computation.73 | convolution fusion | flops 1207959552 | bytes 6291456 | tf_op jit(solution)/shard_map/dot_general | solution.py:149
  117.4 33.3 %all-to-all-done.1 = bf16[8,2,32,3072]{3,2,1,0:T(8,128)(2,1)} async-done(((bf16[8,2,32,3072]{3,2,1,0:T(8,128)(2,1)}), bf16[8,2,32,3072]{3,2,1,0:T(8,128)(2,1)}, u32[]{:S(2)}, u32[]{:S(2)}) %all-to-all-start.1) | async-done | bytes 3145760 | tf_op jit(solution)/shard_map/all_to_all | solution.py:20
  150.7 5.7 %fusion.6 = (bf16[512,384]{1,0:T(8,128)(2,1)S(1)}, f32[512,384]{1,0:T(8,128)}) fusion(f32[512,384]{1,0:T(8,128)S(1)} %fusion.20, bf16[512,3072]{1,0:T(8,128)(2,1)} %bitcast.8, bf16[3072,384]{1,0:T(8,128)(2,1)} %all-gather.3.cloned.1.call-done), kind=kOutput, calls=%fused_computation.16 | convolution fusion | flops 1211891712 | bytes 7471104 | tf_op jit(solution)/shard_map/dot_general | solution.py:146
  156.4 1.8 convolution_convert_fusion
  158.3 7.2 %all_to_all.90 = bf16[2,256,3072]{2,1,0:T(8,128)(2,1)} all-to-all(bf16[2,256,3072]{2,1,0:T(8,128)(2,1)S(1)} %bitcast.92), channel_id=1, replica_groups=mesh['zq'=2,'zp'=2,'y'=4,'x'=4,'zh'=2,'c'=2] {'c'}, dimensions={0} | all-to-all | bytes 6291456 | tf_op jit(solution)/shard_map/all_to_all | solution.py:20
  165.5 2.7 reduce_sum.155
  168.2 24.5 %all_to_all.91 = bf16[4,64,3072]{2,1,0:T(8,128)(2,1)} all-to-all(bf16[4,64,3072]{2,1,0:T(8,128)(2,1)S(1)} %bitcast.90), channel_id=1, replica_groups=mesh['zq'=2,'zp'=2,'y'=4,'x'=4,'zh'=2,'c'=2] {'x'}, dimensions={0} | all-to-all | bytes 3145728 | tf_op jit(solution)/shard_map/all_to_all | solution.py:20
  195.4 9.6 %all-to-all-start.11 = ((bf16[4,32,3072]{2,1,0:T(8,128)(2,1)}), bf16[4,32,3072]{2,1,0:T(8,128)(2,1)S(1)}, u32[]{:S(2)}, u32[]{:S(2)}) async-start(bf16[4,32,3072]{2,1,0:T(8,128)(2,1)} %bitcast.31), calls=%async_computation.11 | async-start | bytes 1572864 | tf_op jit(solution)/shard_map/all_to_all | solution.py:20
  205.7 5.3 %convolution_convert_fusion.2 = bf16[3072,384]{1,0:T(8,128)(2,1)} fusion(bf16[512,3072]{1,0:T(8,128)(2,1)} %bitcast.27, f32[512,384]{1,0:T(8,128)S(1)} %copy-done.17), kind=kOutput, calls=%fused_computation.2 | convolution fusion | flops 1210908672 | bytes 6291456 | tf_op jit(solution)/shard_map/dot_general | solution.py:38
  211.6 5.2 %convolution_convert_fusion.1 = bf16[512,3072]{1,0:T(8,128)(2,1)} fusion(bf16[3072,384]{1,0:T(8,128)(2,1)} %all-gather.5.cloned.1.call-done, f32[512,384]{1,0:T(8,128)S(1)} %copy-done.17), kind=kOutput, calls=%fused_computation.1 | convolution fusion | flops 1211301888 | bytes 6291456 | tf_op jit(solution)/shard_map/dot_general | solution.py:44
  216.8 9.1 %all-to-all-done.11 = bf16[4,32,3072]{2,1,0:T(8,128)(2,1)S(1)} async-done(((bf16[4,32,3072]{2,1,0:T(8,128)(2,1)}), bf16[4,32,3072]{2,1,0:T(8,128)(2,1)S(1)}, u32[]{:S(2)}, u32[]{:S(2)}) %all-to-all-start.11) | async-done | bytes 786464 | tf_op jit(solution)/shard_map/all_to_all | solution.py:20
  226.7 4.0 all-to-all-start.4
  230.7 2.0 convert_reduce_fusion
  232.8 2.2 reshape.360
  235.0 2.0 copy.44
  237.0 2.3 reshape.361
  239.3 1.9 multiply_reduce_fusion.1
  246.1 6.2 %all-to-all-start.15 = ((bf16[16,8,192]{2,1,0:T(8,128)(2,1)}), bf16[16,8,192]{2,1,0:T(8,128)(2,1)}, u32[]{:S(2)}, u32[]{:S(2)}) async-start(bf16[16,8,192]{2,1,0:T(8,128)(2,1)} %bitcast.104), calls=%async_computation.17 | async-start | bytes 131072 | tf_op jit(solution)/shard_map/all_to_all | solution.py:20
  252.3 2.2 reduce_sum.152
  254.5 4.5 %all-to-all-done.15 = bf16[16,8,192]{2,1,0:T(8,128)(2,1)} async-done(((bf16[16,8,192]{2,1,0:T(8,128)(2,1)}), bf16[16,8,192]{2,1,0:T(8,128)(2,1)}, u32[]{:S(2)}, u32[]{:S(2)}) %all-to-all-start.15) | async-done | bytes 49184 | tf_op jit(solution)/shard_map/all_to_all | solution.py:20
  259.0 3.6 all-to-all-start.5
  263.4 19.5 %all-to-all-done.5 = bf16[4,64,3072]{2,1,0:T(8,128)(2,1)S(1)} async-done(((bf16[4,64,3072]{2,1,0:T(8,128)(2,1)}), bf16[4,64,3072]{2,1,0:T(8,128)(2,1)S(1)}, u32[]{:S(2)}, u32[]{:S(2)}) %all-to-all-start.5) | async-done | bytes 1572896 | tf_op jit(solution)/shard_map/all_to_all | solution.py:20
  283.6 5.0 %all-to-all-start.16 = ((bf16[16,8,192]{2,1,0:T(8,128)(2,1)}), bf16[16,8,192]{2,1,0:T(8,128)(2,1)S(1)}, u32[]{:S(2)}, u32[]{:S(2)}) async-start(bf16[16,8,192]{2,1,0:T(8,128)(2,1)} %broadcast_in_dim.87), calls=%async_computation.18 | async-start | bytes 131072 | tf_op jit(solution)/shard_map/all_to_all | solution.py:20
  288.9 6.3 %all-to-all-done.16 = bf16[16,8,192]{2,1,0:T(8,128)(2,1)S(1)} async-done(((bf16[16,8,192]{2,1,0:T(8,128)(2,1)}), bf16[16,8,192]{2,1,0:T(8,128)(2,1)S(1)}, u32[]{:S(2)}, u32[]{:S(2)}) %all-to-all-start.16) | async-done | bytes 49184 | tf_op jit(solution)/shard_map/all_to_all | solution.py:20
  296.2 5.3 %all-to-all-start.6 = ((bf16[4,32,3072]{2,1,0:T(8,128)(2,1)}), bf16[4,32,3072]{2,1,0:T(8,128)(2,1)S(1)}, u32[]{:S(2)}, u32[]{:S(2)}) async-start(bf16[4,32,3072]{2,1,0:T(8,128)(2,1)} %bitcast.19), calls=%async_computation.6 | async-start | bytes 1572864 | tf_op jit(solution)/shard_map/all_to_all | solution.py:20
  301.6 5.2 %convolution_convert_fusion.3 = bf16[3072,384]{1,0:T(8,128)(2,1)} fusion(bf16[512,3072]{1,0:T(8,128)(2,1)} %bitcast.8, bf16[512,384]{1,0:T(8,128)(2,1)S(1)} %copy-done.16), kind=kOutput, calls=%fused_computation.3 | convolution fusion | flops 1209139200 | bytes 5898240 | tf_op jit(solution)/shard_map/dot_general | solution.py:38
  306.9 13.3 %all-to-all-done.6 = bf16[4,32,3072]{2,1,0:T(8,128)(2,1)S(1)} async-done(((bf16[4,32,3072]{2,1,0:T(8,128)(2,1)}), bf16[4,32,3072]{2,1,0:T(8,128)(2,1)S(1)}, u32[]{:S(2)}, u32[]{:S(2)}) %all-to-all-start.6) | async-done | bytes 786464 | tf_op jit(solution)/shard_map/all_to_all | solution.py:20
  320.2 11.5 %all_to_all.92 = bf16[8,8,3072]{2,1,0:T(8,128)(2,1)} all-to-all(bf16[8,8,3072]{2,1,0:T(8,128)(2,1)S(1)} %broadcast_in_dim.89), channel_id=1, replica_groups=mesh['zq'=2,'zp'=2,'y'=4,'x'=4,'zh'=2,'c'=2] {'c','x'}, dimensions={0} | all-to-all | bytes 786432 | tf_op jit(solution)/shard_map/all_to_all | solution.py:20
  333.0 3.6 all-to-all-start.12
  337.8 19.6 %all-to-all-done.12 = bf16[8,32,3072]{2,1,0:T(8,128)(2,1)S(1)} async-done(((bf16[8,32,3072]{2,1,0:T(8,128)(2,1)}), bf16[8,32,3072]{2,1,0:T(8,128)(2,1)S(1)}, u32[]{:S(2)}, u32[]{:S(2)}) %all-to-all-start.12) | async-done | bytes 1572896 | tf_op jit(solution)/shard_map/all_to_all | solution.py:20
  358.9 3.6 all-to-all-start.7
  363.4 19.9 %all-to-all-done.7 = bf16[8,32,3072]{2,1,0:T(8,128)(2,1)S(1)} async-done(((bf16[8,32,3072]{2,1,0:T(8,128)(2,1)}), bf16[8,32,3072]{2,1,0:T(8,128)(2,1)S(1)}, u32[]{:S(2)}, u32[]{:S(2)}) %all-to-all-start.7) | async-done | bytes 1572896 | tf_op jit(solution)/shard_map/all_to_all | solution.py:20
  383.3 4.1 all-to-all-start.14
  388.3 12.7 %all-to-all-done.14 = bf16[4,192,384]{2,1,0:T(8,128)(2,1)} async-done(((bf16[4,192,384]{2,1,0:T(8,128)(2,1)}), bf16[4,192,384]{2,1,0:T(8,128)(2,1)}, u32[]{:S(2)}, u32[]{:S(2)}) %all-to-all-start.14) | async-done | bytes 589856 | tf_op jit(solution)/shard_map/all_to_all | solution.py:20
  401.0 6.2 %all-to-all-start.13 = ((bf16[4,192,384]{2,1,0:T(8,128)(2,1)}), bf16[4,192,384]{2,1,0:T(8,128)(2,1)S(1)}, u32[]{:S(2)}, u32[]{:S(2)}) async-start(bf16[4,192,384]{2,1,0:T(8,128)(2,1)} %bitcast.101), calls=%async_computation.14 | async-start | bytes 1179648 | tf_op jit(solution)/shard_map/all_to_all | solution.py:20
  411.0 8.6 %all-to-all-done.13 = bf16[4,192,384]{2,1,0:T(8,128)(2,1)S(1)} async-done(((bf16[4,192,384]{2,1,0:T(8,128)(2,1)}), bf16[4,192,384]{2,1,0:T(8,128)(2,1)S(1)}, u32[]{:S(2)}, u32[]{:S(2)}) %all-to-all-start.13) | async-done | bytes 589856 | tf_op jit(solution)/shard_map/all_to_all | solution.py:20
  (114 shorter events, 37.0 us)
Async XLA Ops:
  7.2 16.6 %copy-start = (bf16[1,256,3072]{2,1,0:T(8,128)(2,1)S(1)}, bf16[1,256,3072]{2,1,0:T(8,128)(2,1)}, u32[]{:S(2)}) copy-start(bf16[1,256,3072]{2,1,0:T(8,128)(2,1)} %param.17) | copy-start | bytes 4718596
  9.2 18.6 %all-to-all-start.3 = ((bf16[4,192,384]{2,1,0:T(8,128)(2,1)}), bf16[4,192,384]{2,1,0:T(8,128)(2,1)S(1)}, u32[]{:S(2)}, u32[]{:S(2)}) async-start(bf16[4,192,384]{2,1,0:T(8,128)(2,1)} %pad_maximum_fusion.1), calls=%async_computation.3 | async-start | bytes 1179648 | tf_op jit(solution)/shard_map/all_to_all | solution.py:20
  18.7 4.6 %copy-start.10 = (bf16[8,4,4,192]{3,2,1,0:T(4,128)(2,1)}, bf16[8,4,4,192]{3,2,1,0:T(4,128)(2,1)S(1)}, u32[]{:S(2)}) copy-start(bf16[8,4,4,192]{3,2,1,0:T(4,128)(2,1)S(1)} %concatenate.52) | copy-start | bytes 147460
  18.9 5.3 %copy-start.12 = (f32[32]{0:T(128)}, f32[32]{0:T(128)S(1)}, u32[]{:S(2)}) copy-start(f32[32]{0:T(128)S(1)} %broadcast_multiply_fusion.2) | copy-start | bytes 388
  19.1 5.1 %copy-start.13 = (f32[32]{0:T(128)}, f32[32]{0:T(128)S(1)}, u32[]{:S(2)}) copy-start(f32[32]{0:T(128)S(1)} %add_rsqrt_fusion) | copy-start | bytes 388
  27.8 7.9 %copy-start.5 = (bf16[4,192,384]{2,1,0:T(8,128)(2,1)}, bf16[4,192,384]{2,1,0:T(8,128)(2,1)S(1)}, u32[]{:S(2)}) copy-start(bf16[4,192,384]{2,1,0:T(8,128)(2,1)S(1)} %all-to-all-done.3) | copy-start | bytes 1769476
  28.9 15.4 %all-to-all-start = ((bf16[2,2,32,3072]{3,2,1,0:T(8,128)(2,1)}), bf16[2,2,32,3072]{3,2,1,0:T(8,128)(2,1)S(1)}, u32[]{:S(2)}, u32[]{:S(2)}) async-start(bf16[2,2,32,3072]{3,2,1,0:T(8,128)(2,1)} %broadcast_in_dim.36), calls=%async_computation | async-start | bytes 1572864 | tf_op jit(solution)/shard_map/all_to_all | solution.py:20
  35.7 77.3 %all-gather.5.cloned.1.call-start = ((), (), s32[]{:S(2)}) async-start(), calls=%async_computation.21 | async-start | bytes 2949120 | tf_op jit(solution)/shard_map/all_gather | solution.py:64
  44.3 16.5 %all-to-all-start.2 = ((bf16[4,192,384]{2,1,0:T(8,128)(2,1)}), bf16[4,192,384]{2,1,0:T(8,128)(2,1)S(1)}, u32[]{:S(2)}, u32[]{:S(2)}) async-start(bf16[4,192,384]{2,1,0:T(8,128)(2,1)} %pad_maximum_fusion), calls=%async_computation.2 | async-start | bytes 1179648 | tf_op jit(solution)/shard_map/all_to_all | solution.py:20
  60.8 3.2 copy-start.6
  64.0 42.3 %copy-start.7 = (bf16[2,32,3072]{2,1,0:T(8,128)(2,1)S(1)}, bf16[2,32,3072]{2,1,0:T(8,128)(2,1)}, u32[]{:S(2)}) copy-start(bf16[2,32,3072]{2,1,0:T(8,128)(2,1)} %get-tuple-element.19) | copy-start | bytes 1179652
  64.0 42.3 %all-to-all-start.8 = ((bf16[8,2,32,3072]{3,2,1,0:T(8,128)(2,1)}), bf16[8,2,32,3072]{3,2,1,0:T(8,128)(2,1)}, u32[]{:S(2)}, u32[]{:S(2)}) async-start(bf16[8,2,32,3072]{3,2,1,0:T(8,128)(2,1)} %broadcast_in_dim.81), calls=%async_computation.8 | async-start | bytes 6291456 | tf_op jit(solution)/shard_map/all_to_all | solution.py:20
  68.6 82.0 %all-gather.3.cloned.1.call-start = ((), (), s32[]{:S(2)}) async-start(), calls=%async_computation.20 | async-start | bytes 2949120 | tf_op jit(solution)/shard_map/all_gather | solution.py:64
  108.5 42.2 %all-to-all-start.1 = ((bf16[8,2,32,3072]{3,2,1,0:T(8,128)(2,1)}), bf16[8,2,32,3072]{3,2,1,0:T(8,128)(2,1)}, u32[]{:S(2)}, u32[]{:S(2)}) async-start(bf16[8,2,32,3072]{3,2,1,0:T(8,128)(2,1)} %broadcast_in_dim.38), calls=%async_computation.1 | async-start | bytes 6291456 | tf_op jit(solution)/shard_map/all_to_all | solution.py:20
  150.7 5.7 %copy-start.14 = (bf16[3072,384]{1,0:T(8,128)(2,1)S(1)}, bf16[3072,384]{1,0:T(8,128)(2,1)}, u32[]{:S(2)}) copy-start(bf16[3072,384]{1,0:T(8,128)(2,1)} %all-gather.3.cloned.1.call-done) | copy-start | bytes 7077892
  156.4 1.8 copy-start.15
  192.7 13.0 %copy-start.17 = (f32[512,384]{1,0:T(8,128)S(1)}, f32[512,384]{1,0:T(8,128)}, u32[]{:S(2)}) copy-start(f32[512,384]{1,0:T(8,128)} %get-tuple-element.25) | copy-start | bytes 2359300
  195.4 30.5 %all-to-all-start.11 = ((bf16[4,32,3072]{2,1,0:T(8,128)(2,1)}), bf16[4,32,3072]{2,1,0:T(8,128)(2,1)S(1)}, u32[]{:S(2)}, u32[]{:S(2)}) async-start(bf16[4,32,3072]{2,1,0:T(8,128)(2,1)} %bitcast.31), calls=%async_computation.11 | async-start | bytes 1572864 | tf_op jit(solution)/shard_map/all_to_all | solution.py:20
  205.0 178.3 %reduce-scatter.5.cloned.1.call-start = ((), (), s32[]{:S(2)}) async-start(), calls=%async_computation.23 | async-start | bytes 2949120 | tf_op jit(solution)/shard_map/reduce_scatter | solution.py:69
  225.9 0.9 copy-start.4
  226.7 19.4 %all-to-all-start.4 = ((bf16[2,256,3072]{2,1,0:T(8,128)(2,1)}), bf16[2,256,3072]{2,1,0:T(8,128)(2,1)S(1)}, u32[]{:S(2)}, u32[]{:S(2)}) async-start(bf16[2,256,3072]{2,1,0:T(8,128)(2,1)} %bitcast.91), calls=%async_computation.4 | async-start | bytes 6291456 | tf_op jit(solution)/shard_map/all_to_all | solution.py:20
  246.1 12.9 %all-to-all-start.15 = ((bf16[16,8,192]{2,1,0:T(8,128)(2,1)}), bf16[16,8,192]{2,1,0:T(8,128)(2,1)}, u32[]{:S(2)}, u32[]{:S(2)}) async-start(bf16[16,8,192]{2,1,0:T(8,128)(2,1)} %bitcast.104), calls=%async_computation.17 | async-start | bytes 131072 | tf_op jit(solution)/shard_map/all_to_all | solution.py:20
  259.0 23.9 %all-to-all-start.5 = ((bf16[4,64,3072]{2,1,0:T(8,128)(2,1)}), bf16[4,64,3072]{2,1,0:T(8,128)(2,1)S(1)}, u32[]{:S(2)}, u32[]{:S(2)}) async-start(bf16[4,64,3072]{2,1,0:T(8,128)(2,1)} %bitcast.89), calls=%async_computation.5 | async-start | bytes 3145728 | tf_op jit(solution)/shard_map/all_to_all | solution.py:20
  283.6 11.7 %all-to-all-start.16 = ((bf16[16,8,192]{2,1,0:T(8,128)(2,1)}), bf16[16,8,192]{2,1,0:T(8,128)(2,1)S(1)}, u32[]{:S(2)}, u32[]{:S(2)}) async-start(bf16[16,8,192]{2,1,0:T(8,128)(2,1)} %broadcast_in_dim.87), calls=%async_computation.18 | async-start | bytes 131072 | tf_op jit(solution)/shard_map/all_to_all | solution.py:20
  288.6 13.0 %copy-start.16 = (bf16[512,384]{1,0:T(8,128)(2,1)S(1)}, bf16[512,384]{1,0:T(8,128)(2,1)}, u32[]{:S(2)}) copy-start(bf16[512,384]{1,0:T(8,128)(2,1)} %copy-done.15) | copy-start | bytes 1179652
  296.2 24.0 %all-to-all-start.6 = ((bf16[4,32,3072]{2,1,0:T(8,128)(2,1)}), bf16[4,32,3072]{2,1,0:T(8,128)(2,1)S(1)}, u32[]{:S(2)}, u32[]{:S(2)}) async-start(bf16[4,32,3072]{2,1,0:T(8,128)(2,1)} %bitcast.19), calls=%async_computation.6 | async-start | bytes 1572864 | tf_op jit(solution)/shard_map/all_to_all | solution.py:20
  301.6 86.7 %reduce-scatter.3.cloned.1.call-start = ((), (), s32[]{:S(2)}) async-start(), calls=%async_computation.22 | async-start | bytes 2949120 | tf_op jit(solution)/shard_map/reduce_scatter | solution.py:69
  333.0 24.4 %all-to-all-start.12 = ((bf16[8,32,3072]{2,1,0:T(8,128)(2,1)}), bf16[8,32,3072]{2,1,0:T(8,128)(2,1)S(1)}, u32[]{:S(2)}, u32[]{:S(2)}) async-start(bf16[8,32,3072]{2,1,0:T(8,128)(2,1)} %broadcast_in_dim.84), calls=%async_computation.12 | async-start | bytes 3145728 | tf_op jit(solution)/shard_map/all_to_all | solution.py:20
  336.6 1.2 copy-start.11
  337.8 24.7 %copy-start.9 = (bf16[8,8,3072]{2,1,0:T(8,128)(2,1)S(1)}, bf16[8,8,3072]{2,1,0:T(8,128)(2,1)}, u32[]{:S(2)}) copy-start(bf16[8,8,3072]{2,1,0:T(8,128)(2,1)} %all_to_all.92) | copy-start | bytes 1179652
  357.4 30.1 %copy-start.2 = (bf16[8,32,3072]{2,1,0:T(8,128)(2,1)}, bf16[8,32,3072]{2,1,0:T(8,128)(2,1)S(1)}, u32[]{:S(2)}) copy-start(bf16[8,32,3072]{2,1,0:T(8,128)(2,1)S(1)} %all-to-all-done.12) | copy-start | bytes 4718596
  358.9 24.4 %all-to-all-start.7 = ((bf16[8,32,3072]{2,1,0:T(8,128)(2,1)}), bf16[8,32,3072]{2,1,0:T(8,128)(2,1)S(1)}, u32[]{:S(2)}, u32[]{:S(2)}) async-start(bf16[8,32,3072]{2,1,0:T(8,128)(2,1)} %broadcast_in_dim.78), calls=%async_computation.7 | async-start | bytes 3145728 | tf_op jit(solution)/shard_map/all_to_all | solution.py:20
  383.3 4.2 copy-start.3
  383.3 17.7 %all-to-all-start.14 = ((bf16[4,192,384]{2,1,0:T(8,128)(2,1)}), bf16[4,192,384]{2,1,0:T(8,128)(2,1)}, u32[]{:S(2)}, u32[]{:S(2)}) async-start(bf16[4,192,384]{2,1,0:T(8,128)(2,1)} %bitcast.100), calls=%async_computation.16 | async-start | bytes 1179648 | tf_op jit(solution)/shard_map/all_to_all | solution.py:20
  387.5 19.7 %slice-start = ((bf16[8,32,3072]{2,1,0:T(8,128)(2,1)}), bf16[8,24,3072]{2,1,0:T(8,128)(2,1)S(1)}, s32[]{:S(2)}) async-start(bf16[8,32,3072]{2,1,0:T(8,128)(2,1)} %copy-done.2), calls=%async_computation.24 | async-start | bytes 2359296 | tf_op jit(solution)/shard_map/slice | solution.py:88
  388.3 20.2 %slice-start.1 = ((bf16[8,32,3072]{2,1,0:T(8,128)(2,1)}), bf16[8,24,3072]{2,1,0:T(8,128)(2,1)S(1)}, s32[]{:S(2)}) async-start(bf16[8,32,3072]{2,1,0:T(8,128)(2,1)} %copy-done.3), calls=%async_computation.25 | async-start | bytes 2359296 | tf_op jit(solution)/shard_map/slice | solution.py:88
  401.0 18.7 %all-to-all-start.13 = ((bf16[4,192,384]{2,1,0:T(8,128)(2,1)}), bf16[4,192,384]{2,1,0:T(8,128)(2,1)S(1)}, u32[]{:S(2)}, u32[]{:S(2)}) async-start(bf16[4,192,384]{2,1,0:T(8,128)(2,1)} %bitcast.101), calls=%async_computation.14 | async-start | bytes 1179648 | tf_op jit(solution)/shard_map/all_to_all | solution.py:20
  407.2 1.3 copy-start.8
  409.7 11.1 %copy-start.1 = (bf16[1,256,3072]{2,1,0:T(8,128)(2,1)S(1)}, bf16[1,256,3072]{2,1,0:T(8,128)(2,1)}, u32[]{:S(2)}) copy-start(bf16[1,256,3072]{2,1,0:T(8,128)(2,1)} %param.17) | copy-start | bytes 4718596
Sparse Core Ops, SparseCore 0:
  38.9 36.4 all-gather.4
  77.7 35.5 all-gather.2
  211.1 33.8 reduce-scatter.4
  306.9 31.5 reduce-scatter.2
